TPU v7x, 32 devices: a whole 2x2x4 slice. The times are simulated.
32 devices in a mesh: gx: 2 (over core), gyz: 16 (over z, y, x).
Axes of the slice: x: 2, y: 2, z: 4, core: 2. Of those that a mesh axis runs over, the one named last changes fastest.
Arguments:
- bands: bfloat16 [16, 80, 40, 512], P('gx', 'gyz'), may hold values from -6 to 6
- potential: float32 [16, 80, 40], P('gx', 'gyz'), may hold values from 0.5 to 4
- eigenvectors: bfloat16 [512, 512], P('gyz'), may hold values from -0.25 to 0.25
Outputs:
- correlation: float32 [512, 512], P('gyz')
- hamiltonian: float32 [512, 512], P('gyz')
- rotated: bfloat16 [16, 80, 40, 512], P('gx', 'gyz')
All inputs are finite; a program needn't handle non-finite values.
Results may differ from a plain program's by a relative error of at most 0.0012.
Values may be sent and summed in bfloat16 or wider, within the bound.
A program may use at most 64 MiB of HBM per device.

v0:
```python
import jax
import jax.numpy as jnp
from jax import lax
from jax.sharding import PartitionSpec as P


def extended(block, sides, width):
    for axis, dim in sides:
        count = lax.axis_size(axis)
        forward = [(i, i + 1) for i in range(count - 1)]
        backward = [(target, source) for source, target in forward]
        low = lax.ppermute(
            lax.slice_in_dim(block, block.shape[dim] - width, None, axis=dim), axis, forward
        )
        high = lax.ppermute(lax.slice_in_dim(block, 0, width, axis=dim), axis, backward)
        block = jnp.concatenate([low, block, high], axis=dim)
    return block


def stencil(padded, potential):
    centre = padded[1:-1, 1:-1, 1:-1].astype(jnp.float32)
    neighbours = padded[2:, 1:-1, 1:-1].astype(jnp.float32) + padded[:-2, 1:-1, 1:-1].astype(
        jnp.float32
    )
    neighbours = (
        neighbours
        + padded[1:-1, 2:, 1:-1].astype(jnp.float32)
        + padded[1:-1, :-2, 1:-1].astype(jnp.float32)
    )
    neighbours = (
        neighbours
        + padded[1:-1, 1:-1, 2:].astype(jnp.float32)
        + padded[1:-1, 1:-1, :-2].astype(jnp.float32)
    )
    return ((3.0 + potential[..., None]) * centre - 0.5 * neighbours).astype(jnp.bfloat16)


def on_device(bands, potential, eigenvectors):
    halo_bands = extended(bands, (("gx", 0), ("gyz", 1)), 1)
    padded = jnp.pad(halo_bands, ((0, 0), (0, 0), (1, 1), (0, 0)))
    hamil_bands = stencil(padded, potential)
    band_count = bands.shape[3]
    cell_count = bands.shape[0] * bands.shape[1] * bands.shape[2]
    flat_bands = bands.reshape(cell_count, band_count)
    combined = jnp.concatenate((flat_bands, hamil_bands.reshape(cell_count, band_count)), axis=1)
    inv_volume = 1.0 / (cell_count * lax.axis_size("gyz"))
    product = lax.dot_general(
        flat_bands, combined, (((0,), (0,)), ((), ())), preferred_element_type=jnp.float32
    )
    row_terms = lax.psum_scatter(product * inv_volume, "gyz", scatter_dimension=0, tiled=True)
    gram_block = lax.psum(row_terms, "gx")
    coefficients = lax.all_gather(eigenvectors, "gyz", axis=0, tiled=True)
    rotated = jnp.dot(flat_bands, coefficients, preferred_element_type=jnp.float32)
    return (
        gram_block[:, :band_count],
        gram_block[:, band_count:],
        rotated.astype(jnp.bfloat16).reshape(bands.shape),
    )


def solution(mesh):
    in_specs = (P("gx", "gyz", None, None), P("gx", "gyz", None), P("gyz", None))
    out_specs = (P("gyz", None), P("gyz", None), P("gx", "gyz", None, None))
    return jax.shard_map(
        on_device, mesh=mesh, in_specs=in_specs, out_specs=out_specs, check_vma=False
    )
```

profile of v0, /device:TPU:0, one launch (start us, length us, event | category | flops | bytes accessed | tf_op | source)
XLA Modules:
  0.0 162.3 jit_solution(2966103501217675455)
XLA Ops:
  7.2 0.0 reduce-scatter.4.cloned.1.call-start
  7.2 1.1 fusion.14
  8.3 2.4 %collective-permute-start.1 = (bf16[1,5,40,512]{3,2,1,0:T(8,128)(2,1)S(1)}, bf16[1,5,40,512]{3,2,1,0:T(8,128)(2,1)S(1)}, u32[]{:S(2)}, u32[]{:S(2)}) collective-permute-start(bf16[1,5,40,512]{3,2,1,0:T(8,128)(2,1)S(1)} %get-tuple-element.12), channel_id=1, source_target_pairs={{0,16},{1,17},{2,18},{3,19},{4,20},{5,21},{6,22},{7,23},{8,24},{9,... | collective-permute-start | bytes 614408 | tf_op jit(solution)/shard_map/ppermute | solution.py:12
  10.7 1.3 collective-permute-start
  12.0 0.0 collective-permute-done.1
  12.0 0.0 copy-start.2
  12.0 1.5 constant_dynamic-update-slice_fusion.1
  13.6 0.5 collective-permute-done
  14.1 0.1 fusion.13
  14.1 1.3 collective-permute-start.2
  15.4 4.9 %collective-permute-start.3 = (bf16[10,1,40,512]{3,2,1,0:T(8,128)(2,1)S(1)}, bf16[10,1,40,512]{3,2,1,0:T(8,128)(2,1)S(1)}, u32[]{:S(2)}, u32[]{:S(2)}) collective-permute-start(bf16[10,1,40,512]{3,2,1,0:T(8,128)(2,1)S(1)} %get-tuple-element.9), channel_id=1, source_target_pairs={{0,1},{1,2},{2,3},{3,4},{4,5},{5,6},{6,7},{7,8},{8,9},{9,10},{10,1... | collective-permute-start | bytes 1228808 | tf_op jit(solution)/shard_map/ppermute | solution.py:12
  20.3 0.0 copy-done.2
  20.3 0.0 copy-start
  20.3 8.3 %collective-permute-done.2 = bf16[10,1,40,512]{3,2,1,0:T(8,128)(2,1)S(1)} collective-permute-done((bf16[10,1,40,512]{3,2,1,0:T(8,128)(2,1)S(1)}, bf16[10,1,40,512]{3,2,1,0:T(8,128)(2,1)S(1)}, u32[]{:S(2)}, u32[]{:S(2)}) %collective-permute-start.2) | collective-permute-done | bytes 409632 | tf_op jit(solution)/shard_map/ppermute | solution.py:15
  28.6 9.9 %collective-permute-done.3 = bf16[10,1,40,512]{3,2,1,0:T(8,128)(2,1)S(1)} collective-permute-done((bf16[10,1,40,512]{3,2,1,0:T(8,128)(2,1)S(1)}, bf16[10,1,40,512]{3,2,1,0:T(8,128)(2,1)S(1)}, u32[]{:S(2)}, u32[]{:S(2)}) %collective-permute-start.3) | collective-permute-done | bytes 409632 | tf_op jit(solution)/shard_map/ppermute | solution.py:12
  38.6 1.7 %fusion.5 = bf16[10,7,42,512]{3,2,1,0:T(8,128)(2,1)S(1)} fusion(bf16[10,1,40,512]{3,2,1,0:T(8,128)(2,1)S(1)} %collective-permute-done.2, bf16[10,5,40,512]{3,2,1,0:T(8,128)(2,1)S(1)} %constant_dynamic-update-slice_fusion, bf16[10,1,40,512]{3,2,1,0:T(8,128)(2,1)S(1)} %collective-permute-done.3), kind=kLoop, calls=%fused_computation.7 | loop fusion | flops 18063360 | bytes 5877760 | tf_op jit(solution)/shard_map/concatenate | solution.py:16
  40.3 0.0 copy-done
  40.3 3.3 %subtract_convert_fusion = bf16[8,5,40,512]{3,2,1,0:T(8,128)(2,1)S(1)} fusion(bf16[8,5,40,512]{3,2,1,0:T(8,128)(2,1)S(1)} %copy-done, bf16[10,7,42,512]{3,2,1,0:T(8,128)(2,1)S(1)} %fusion.5, bf16[10,5,40,512]{3,2,1,0:T(8,128)(2,1)S(1)} %constant_dynamic-update-slice_fusion, bf16[10,1,40,512]{3,2,1,0:T(8,128)(2,1)S(1)} %collective-permute-done.3, ...), kind=kLoop, calls=%fused_computation.12 | loop fusion | flops 16384000 | bytes 9836800 | tf_op jit(solution)/shard_map/convert_element_type | solution.py:35
  43.6 3.4 %multiply_bitcast_fusion = f32[512,1024]{0,1:T(8,128)} fusion(bf16[1600,512]{1,0:T(8,128)(2,1)S(1)} %bitcast.9, bf16[1600,512]{1,0:T(8,128)(2,1)S(1)} %bitcast.11), kind=kOutput, calls=%fused_computation.14 | convolution fusion | flops 1684799488 | bytes 5373952 | tf_op jit(solution)/shard_map/dot_general | solution.py:47
  47.0 2.9 %copy.12 = f32[512,1024]{1,0:T(8,128)} copy(f32[512,1024]{0,1:T(8,128)} %multiply_bitcast_fusion) | data formatting | bytes 4194304
  50.0 0.0 copy-start.1
  50.0 0.0 reduce-scatter.4.cloned.1.call-update
  50.0 0.0 all-reduce.3.cloned.1.call-start
  50.0 0.7 copy-done.1
  50.7 46.1 %all_gather.3 = bf16[512,512]{1,0:T(8,128)(2,1)S(1)} all-gather(bf16[32,512]{1,0:T(8,128)(2,1)S(1)} %copy-done.1), channel_id=1, replica_groups=mesh['gx'=2,'gyz'=16] {'gyz'}, dimensions={0}, use_global_device_ids=true | all-gather | bytes 557056 | tf_op jit(solution)/shard_map/all_gather | solution.py:52
  96.9 36.3 %reduce-scatter.4.cloned.1.call-done = f32[32,1024]{1,0:T(8,128)} async-done(((f32[512,1024]{1,0:T(8,128)}), f32[32,1024]{1,0:T(8,128)}) %reduce-scatter.4.cloned.1.call-update) | async-done | bytes 131088
  133.1 1.9 %copy.13 = f32[32,1024]{0,1:T(8,128)} copy(f32[32,1024]{1,0:T(8,128)} %reduce-scatter.4.cloned.1.call-done) | data formatting | bytes 262144
  135.1 0.0 all-reduce.3.cloned.1.call-update
  135.1 2.2 %convolution_convert_fusion = bf16[1600,512]{1,0:T(8,128)(2,1)} fusion(bf16[1600,512]{1,0:T(8,128)(2,1)S(1)} %bitcast.10, bf16[512,512]{1,0:T(8,128)(2,1)S(1)} %all_gather.3), kind=kOutput, calls=%fused_computation.13 | convolution fusion | flops 839680000 | bytes 3801088 | tf_op jit(solution)/shard_map/dot_general | solution.py:53
  137.3 15.7 %all-reduce.3.cloned.1.call-done = f32[32,1024]{0,1:T(8,128)} async-done(((f32[32,1024]{0,1:T(8,128)}), f32[32,1024]{0,1:T(8,128)}) %all-reduce.3.cloned.1.call-update) | async-done | bytes 131088 | tf_op jit(solution)/shard_map/psum | solution.py:51
  152.9 1.1 fusion.15
  154.0 0.7 copy.10
  154.7 0.7 copy.11
  (4 shorter events, 0.0 us)
Async XLA Ops:
  7.2 126.0 %reduce-scatter.4.cloned.1.call-start = ((), (), s32[]{:S(2)}) async-start(), calls=%async_computation.2 | async-start | bytes 2228224
  8.3 3.7 %collective-permute-start.1 = (bf16[1,5,40,512]{3,2,1,0:T(8,128)(2,1)S(1)}, bf16[1,5,40,512]{3,2,1,0:T(8,128)(2,1)S(1)}, u32[]{:S(2)}, u32[]{:S(2)}) collective-permute-start(bf16[1,5,40,512]{3,2,1,0:T(8,128)(2,1)S(1)} %get-tuple-element.12), channel_id=1, source_target_pairs={{0,16},{1,17},{2,18},{3,19},{4,20},{5,21},{6,22},{7,23},{8,24},{9,... | collective-permute-start | bytes 614408 | tf_op jit(solution)/shard_map/ppermute | solution.py:12
  10.7 3.3 %collective-permute-start = (bf16[1,5,40,512]{3,2,1,0:T(8,128)(2,1)S(1)}, bf16[1,5,40,512]{3,2,1,0:T(8,128)(2,1)S(1)}, u32[]{:S(2)}, u32[]{:S(2)}) collective-permute-start(bf16[1,5,40,512]{3,2,1,0:T(8,128)(2,1)S(1)} %get-tuple-element.11), channel_id=1, source_target_pairs={{16,0},{17,1},{18,2},{19,3},{20,4},{21,5},{22,6},{23,7},{24,8},{25... | collective-permute-start | bytes 614408 | tf_op jit(solution)/shard_map/ppermute | solution.py:15
  12.0 8.3 %copy-start.2 = (f32[8,5,40]{2,0,1:T(8,128)S(1)}, f32[8,5,40]{2,0,1:T(8,128)}, u32[]{:S(2)}) copy-start(f32[8,5,40]{2,0,1:T(8,128)} %param.4) | copy-start | bytes 19204
  14.1 14.5 %collective-permute-start.2 = (bf16[10,1,40,512]{3,2,1,0:T(8,128)(2,1)S(1)}, bf16[10,1,40,512]{3,2,1,0:T(8,128)(2,1)S(1)}, u32[]{:S(2)}, u32[]{:S(2)}) collective-permute-start(bf16[10,1,40,512]{3,2,1,0:T(8,128)(2,1)S(1)} %get-tuple-element.10), channel_id=1, source_target_pairs={{1,0},{2,1},{3,2},{4,3},{5,4},{6,5},{7,6},{8,7},{9,8},{10,9},{11,1... | collective-permute-start | bytes 1228808 | tf_op jit(solution)/shard_map/ppermute | solution.py:15
  15.4 23.1 %collective-permute-start.3 = (bf16[10,1,40,512]{3,2,1,0:T(8,128)(2,1)S(1)}, bf16[10,1,40,512]{3,2,1,0:T(8,128)(2,1)S(1)}, u32[]{:S(2)}, u32[]{:S(2)}) collective-permute-start(bf16[10,1,40,512]{3,2,1,0:T(8,128)(2,1)S(1)} %get-tuple-element.9), channel_id=1, source_target_pairs={{0,1},{1,2},{2,3},{3,4},{4,5},{5,6},{6,7},{7,8},{8,9},{9,10},{10,1... | collective-permute-start | bytes 1228808 | tf_op jit(solution)/shard_map/ppermute | solution.py:12
  20.3 19.9 %copy-start = (bf16[8,5,40,512]{3,2,1,0:T(8,128)(2,1)S(1)}, bf16[8,5,40,512]{3,2,1,0:T(8,128)(2,1)}, u32[]{:S(2)}) copy-start(bf16[8,5,40,512]{3,2,1,0:T(8,128)(2,1)} %param.3) | copy-start | bytes 4915204
  50.0 0.8 copy-start.1
  50.0 102.9 %all-reduce.3.cloned.1.call-start = ((), (), s32[]{:S(2)}) async-start(), calls=%async_computation.1 | async-start | bytes 1048576 | tf_op jit(solution)/shard_map/psum | solution.py:51
Sparse Core Ops, SparseCore 0:
  50.1 82.9 reduce-scatter.3
  135.5 17.3 all-reduce.2
where the time goes:
time: 163 us; the launch traced here: 162 us
  waiting for transfers between devices  70.7 us (43%)
  blocking collectives  46.1 us (28%)
  between operations  14.2 us (9%)
  local copies, waits for them, and re-layouts  10.8 us (7%)
  starting transfers between devices  9.94 us (6%)
  matrix products  5.59 us (3%)
  other arithmetic  5.03 us (3%)
    all_gather x1, blocking collectives, on_device(): coefficients = lax.all_gather(eigenvectors, 'gyz', axis=0, tiled=True)  46.1 us
    unnamed x3, waiting for transfers between devices  36.3 us
    psum x1, waiting for transfers between devices, on_device(): gram_block = lax.psum(row_terms, 'gx')  15.7 us
    ppermute x2, waiting for transfers between devices, extended(): lax.ppermute(lax.slice_in_dim(block, block.shape[dim] - width, None, axis...  9.91 us
    ppermute x2, waiting for transfers between devices, extended(): lax.ppermute(lax.slice_in_dim(block, 0, width, axis=dim), axis, backward)  8.75 us
    unnamed x12, local copies, waits for them, and re-layouts  8.56 us
    ppermute x2, starting transfers between devices, extended(): lax.ppermute(lax.slice_in_dim(block, block.shape[dim] - width, None, axis...  7.28 us
    dot_general x1, matrix products, on_device(): lax.dot_general(flat_bands, combined, (((0,), (0,)), ((), ())), preferred...  3.41 us
  transfers between devices with their start and end apart: 6, of which 5 were waited for; matrix products, arithmetic and copies ran while one was open for 2% of the time, Pallas kernels for 0%

commit v1 on v0

--- a/solution.py
+++ b/solution.py
@@ -48,7 +48,7 @@
         flat_bands, combined, (((0,), (0,)), ((), ())), preferred_element_type=jnp.float32
     )
     row_terms = lax.psum_scatter(product * inv_volume, "gyz", scatter_dimension=0, tiled=True)
-    gram_block = lax.psum(row_terms, "gx")
+    gram_block = jnp.sum(lax.all_gather(row_terms, "gx"), axis=0)
     coefficients = lax.all_gather(eigenvectors, "gyz", axis=0, tiled=True)
     rotated = jnp.dot(flat_bands, coefficients, preferred_element_type=jnp.float32)
     return (

time: 163 us -> 143 us (0.88)
  waiting for transfers between devices: 70.7 us -> 52.8 us
  local copies, waits for them, and re-layouts: 10.8 us -> 7.05 us
  blocking collectives: 46.1 us -> 48.3 us
    unnamed x3 -> x1, waiting for transfers between devices: 36.3 us -> 0.02 us
    reduce_scatter x0 -> x1, waiting for transfers between devices: none -> 34.1 us  [on_device(): lax.psum_scatter(product * inv_volume, 'gyz', scatter_dimension=0, tiled=...]
    psum x1 -> x0, waiting for transfers between devices: 15.7 us -> none  [on_device(): gram_block = lax.psum(row_terms, 'gx')]
    unnamed x12 -> x9, local copies, waits for them, and re-layouts: 8.56 us -> 5.24 us
    all_gather x0 -> x1, blocking collectives: none -> 2.19 us  [on_device(): gram_block = jnp.sum(lax.all_gather(row_terms, 'gx'), axis=0)]
  transfers between devices with their start and end apart: 6 -> 5, of which waited for: 5 -> 4; matrix products, arithmetic and copies ran while one was open for 2% -> 3% of each run, Pallas kernels for 0% -> 0%
where the time goes in v1:
time: 143 us
  waiting for transfers between devices  52.8 us (37%)
  blocking collectives  48.3 us (34%)
  between operations  14.2 us (10%)
  starting transfers between devices  9.9 us (7%)
  local copies, waits for them, and re-layouts  7.05 us (5%)
  matrix products  5.58 us (4%)
  other arithmetic  5.05 us (4%)
    all_gather x1, blocking collectives, on_device(): coefficients = lax.all_gather(eigenvectors, 'gyz', axis=0, tiled=True)  46.1 us
    reduce_scatter x1, waiting for transfers between devices, on_device(): lax.psum_scatter(product * inv_volume, 'gyz', scatter_dimension=0, tiled=...  34.1 us
    ppermute x2, waiting for transfers between devices, extended(): lax.ppermute(lax.slice_in_dim(block, block.shape[dim] - width, None, axis...  9.91 us
    ppermute x2, waiting for transfers between devices, extended(): lax.ppermute(lax.slice_in_dim(block, 0, width, axis=dim), axis, backward)  8.75 us
    ppermute x2, starting transfers between devices, extended(): lax.ppermute(lax.slice_in_dim(block, block.shape[dim] - width, None, axis...  7.28 us
    unnamed x9, local copies, waits for them, and re-layouts  5.24 us
    dot_general x1, matrix products, on_device(): lax.dot_general(flat_bands, combined, (((0,), (0,)), ((), ())), preferred...  3.4 us
    convert_element_type x1, other arithmetic, stencil(): ((3.0 + potential[..., None]) * centre - 0.5 * neighbours).astype(jnp.bfl...  3.31 us
  transfers between devices with their start and end apart: 5, of which 4 were waited for; matrix products, arithmetic and copies ran while one was open for 3% of the time, Pallas kernels for 0%

profile of v1, /device:TPU:0, one launch (start us, length us, event | category | flops | bytes accessed | tf_op | source)
XLA Modules:
  0.0 142.9 jit_solution(3110116249896776504)
XLA Ops:
  7.2 0.0 reduce-scatter.4.cloned.1.call-start
  7.2 1.1 fusion.14
  8.3 2.4 %collective-permute-start.1 = (bf16[1,5,40,512]{3,2,1,0:T(8,128)(2,1)S(1)}, bf16[1,5,40,512]{3,2,1,0:T(8,128)(2,1)S(1)}, u32[]{:S(2)}, u32[]{:S(2)}) collective-permute-start(bf16[1,5,40,512]{3,2,1,0:T(8,128)(2,1)S(1)} %get-tuple-element.6), channel_id=1, source_target_pairs={{0,16},{1,17},{2,18},{3,19},{4,20},{5,21},{6,22},{7,23},{8,24},{9,... | collective-permute-start | bytes 614408 | tf_op jit(solution)/shard_map/ppermute | solution.py:12
  10.7 1.3 collective-permute-start
  12.0 0.0 collective-permute-done.1
  12.0 0.0 copy-start.2
  12.0 1.5 %constant_dynamic-update-slice_fusion.1 = bf16[10,5,40,512]{3,2,1,0:T(8,128)(2,1)S(1)} fusion(bf16[10,5,40,512]{3,2,1,0:T(8,128)(2,1)S(1)} %constant_dynamic-update-slice_fusion.2, bf16[8,5,40,512]{3,2,1,0:T(8,128)(2,1)} %param.3), kind=kLoop, calls=%fused_computation.21 | loop fusion | bytes 3276800
  13.6 0.5 collective-permute-done
  14.1 0.1 fusion.13
  14.1 1.3 collective-permute-start.2
  15.4 4.9 %collective-permute-start.3 = (bf16[10,1,40,512]{3,2,1,0:T(8,128)(2,1)S(1)}, bf16[10,1,40,512]{3,2,1,0:T(8,128)(2,1)S(1)}, u32[]{:S(2)}, u32[]{:S(2)}) collective-permute-start(bf16[10,1,40,512]{3,2,1,0:T(8,128)(2,1)S(1)} %get-tuple-element.3), channel_id=1, source_target_pairs={{0,1},{1,2},{2,3},{3,4},{4,5},{5,6},{6,7},{7,8},{8,9},{9,10},{10,1... | collective-permute-start | bytes 1228808 | tf_op jit(solution)/shard_map/ppermute | solution.py:12
  20.3 0.0 copy-done.2
  20.3 0.0 copy-start
  20.3 8.3 %collective-permute-done.2 = bf16[10,1,40,512]{3,2,1,0:T(8,128)(2,1)S(1)} collective-permute-done((bf16[10,1,40,512]{3,2,1,0:T(8,128)(2,1)S(1)}, bf16[10,1,40,512]{3,2,1,0:T(8,128)(2,1)S(1)}, u32[]{:S(2)}, u32[]{:S(2)}) %collective-permute-start.2) | collective-permute-done | bytes 409632 | tf_op jit(solution)/shard_map/ppermute | solution.py:15
  28.6 9.9 %collective-permute-done.3 = bf16[10,1,40,512]{3,2,1,0:T(8,128)(2,1)S(1)} collective-permute-done((bf16[10,1,40,512]{3,2,1,0:T(8,128)(2,1)S(1)}, bf16[10,1,40,512]{3,2,1,0:T(8,128)(2,1)S(1)}, u32[]{:S(2)}, u32[]{:S(2)}) %collective-permute-start.3) | collective-permute-done | bytes 409632 | tf_op jit(solution)/shard_map/ppermute | solution.py:12
  38.6 1.7 %fusion.5 = bf16[10,7,42,512]{3,2,1,0:T(8,128)(2,1)S(1)} fusion(bf16[10,1,40,512]{3,2,1,0:T(8,128)(2,1)S(1)} %collective-permute-done.2, bf16[10,5,40,512]{3,2,1,0:T(8,128)(2,1)S(1)} %constant_dynamic-update-slice_fusion, bf16[10,1,40,512]{3,2,1,0:T(8,128)(2,1)S(1)} %collective-permute-done.3), kind=kLoop, calls=%fused_computation.7 | loop fusion | flops 18063360 | bytes 5877760 | tf_op jit(solution)/shard_map/concatenate | solution.py:16
  40.3 0.0 copy-done
  40.3 3.3 %subtract_convert_fusion = bf16[8,5,40,512]{3,2,1,0:T(8,128)(2,1)S(1)} fusion(bf16[8,5,40,512]{3,2,1,0:T(8,128)(2,1)S(1)} %copy-done, bf16[10,7,42,512]{3,2,1,0:T(8,128)(2,1)S(1)} %fusion.5, bf16[10,5,40,512]{3,2,1,0:T(8,128)(2,1)S(1)} %constant_dynamic-update-slice_fusion, bf16[10,1,40,512]{3,2,1,0:T(8,128)(2,1)S(1)} %collective-permute-done.3, ...), kind=kLoop, calls=%fused_computation.12 | loop fusion | flops 16384000 | bytes 9836800 | tf_op jit(solution)/shard_map/convert_element_type | solution.py:35
  43.6 3.4 %multiply_bitcast_fusion = f32[512,1024]{0,1:T(8,128)} fusion(bf16[1600,512]{1,0:T(8,128)(2,1)S(1)} %bitcast.10, bf16[1600,512]{1,0:T(8,128)(2,1)S(1)} %bitcast.12), kind=kOutput, calls=%fused_computation.14 | convolution fusion | flops 1684799488 | bytes 5373952 | tf_op jit(solution)/shard_map/dot_general | solution.py:47
  47.0 2.9 %copy.11 = f32[512,1024]{1,0:T(8,128)} copy(f32[512,1024]{0,1:T(8,128)} %multiply_bitcast_fusion) | data formatting | bytes 4194304
  50.0 0.0 copy-start.1
  50.0 0.0 reduce-scatter.4.cloned.1.call-update
  50.0 0.7 copy-done.1
  50.7 46.1 %all_gather.11 = bf16[512,512]{1,0:T(8,128)(2,1)S(1)} all-gather(bf16[32,512]{1,0:T(8,128)(2,1)S(1)} %copy-done.1), channel_id=1, replica_groups=mesh['gx'=2,'gyz'=16] {'gyz'}, dimensions={0}, use_global_device_ids=true | all-gather | bytes 557056 | tf_op jit(solution)/shard_map/all_gather | solution.py:52
  96.9 2.2 %convolution_convert_fusion = bf16[1600,512]{1,0:T(8,128)(2,1)} fusion(bf16[1600,512]{1,0:T(8,128)(2,1)S(1)} %bitcast.11, bf16[512,512]{1,0:T(8,128)(2,1)S(1)} %all_gather.11), kind=kOutput, calls=%fused_computation.13 | convolution fusion | flops 839680000 | bytes 3801088 | tf_op jit(solution)/shard_map/dot_general | solution.py:53
  99.0 34.1 %reduce-scatter.4.cloned.1.call-done = f32[32,1024]{1,0:T(8,128)} async-done(((f32[512,1024]{1,0:T(8,128)}), f32[32,1024]{1,0:T(8,128)}) %reduce-scatter.4.cloned.1.call-update) | async-done | bytes 131088 | tf_op jit(solution)/shard_map/reduce_scatter | solution.py:50
  133.1 2.2 %all-gather = f32[64,1024]{1,0:T(8,128)S(1)} all-gather(f32[32,1024]{1,0:T(8,128)} %reduce-scatter.4.cloned.1.call-done), channel_id=2, replica_groups=mesh['gx'=2,'gyz'=16] {'gx'}, dimensions={0}, use_global_device_ids=true | all-gather | bytes 393216 | tf_op jit(solution)/shard_map/all_gather | solution.py:51
  135.4 0.7 fusion.15
  (5 shorter events, 0.1 us)
Async XLA Ops:
  7.2 126.0 %reduce-scatter.4.cloned.1.call-start = ((), (), s32[]{:S(2)}) async-start(), calls=%async_computation.1 | async-start | bytes 2228224 | tf_op jit(solution)/shard_map/reduce_scatter | solution.py:50
  8.3 3.7 %collective-permute-start.1 = (bf16[1,5,40,512]{3,2,1,0:T(8,128)(2,1)S(1)}, bf16[1,5,40,512]{3,2,1,0:T(8,128)(2,1)S(1)}, u32[]{:S(2)}, u32[]{:S(2)}) collective-permute-start(bf16[1,5,40,512]{3,2,1,0:T(8,128)(2,1)S(1)} %get-tuple-element.6), channel_id=1, source_target_pairs={{0,16},{1,17},{2,18},{3,19},{4,20},{5,21},{6,22},{7,23},{8,24},{9,... | collective-permute-start | bytes 614408 | tf_op jit(solution)/shard_map/ppermute | solution.py:12
  10.7 3.3 %collective-permute-start = (bf16[1,5,40,512]{3,2,1,0:T(8,128)(2,1)S(1)}, bf16[1,5,40,512]{3,2,1,0:T(8,128)(2,1)S(1)}, u32[]{:S(2)}, u32[]{:S(2)}) collective-permute-start(bf16[1,5,40,512]{3,2,1,0:T(8,128)(2,1)S(1)} %get-tuple-element.5), channel_id=1, source_target_pairs={{16,0},{17,1},{18,2},{19,3},{20,4},{21,5},{22,6},{23,7},{24,8},{25... | collective-permute-start | bytes 614408 | tf_op jit(solution)/shard_map/ppermute | solution.py:15
  12.0 8.3 %copy-start.2 = (f32[8,5,40]{2,0,1:T(8,128)S(1)}, f32[8,5,40]{2,0,1:T(8,128)}, u32[]{:S(2)}) copy-start(f32[8,5,40]{2,0,1:T(8,128)} %param.4) | copy-start | bytes 19204
  14.1 14.5 %collective-permute-start.2 = (bf16[10,1,40,512]{3,2,1,0:T(8,128)(2,1)S(1)}, bf16[10,1,40,512]{3,2,1,0:T(8,128)(2,1)S(1)}, u32[]{:S(2)}, u32[]{:S(2)}) collective-permute-start(bf16[10,1,40,512]{3,2,1,0:T(8,128)(2,1)S(1)} %get-tuple-element.4), channel_id=1, source_target_pairs={{1,0},{2,1},{3,2},{4,3},{5,4},{6,5},{7,6},{8,7},{9,8},{10,9},{11,1... | collective-permute-start | bytes 1228808 | tf_op jit(solution)/shard_map/ppermute | solution.py:15
  15.4 23.1 %collective-permute-start.3 = (bf16[10,1,40,512]{3,2,1,0:T(8,128)(2,1)S(1)}, bf16[10,1,40,512]{3,2,1,0:T(8,128)(2,1)S(1)}, u32[]{:S(2)}, u32[]{:S(2)}) collective-permute-start(bf16[10,1,40,512]{3,2,1,0:T(8,128)(2,1)S(1)} %get-tuple-element.3), channel_id=1, source_target_pairs={{0,1},{1,2},{2,3},{3,4},{4,5},{5,6},{6,7},{7,8},{8,9},{9,10},{10,1... | collective-permute-start | bytes 1228808 | tf_op jit(solution)/shard_map/ppermute | solution.py:12
  20.3 19.9 %copy-start = (bf16[8,5,40,512]{3,2,1,0:T(8,128)(2,1)S(1)}, bf16[8,5,40,512]{3,2,1,0:T(8,128)(2,1)}, u32[]{:S(2)}) copy-start(bf16[8,5,40,512]{3,2,1,0:T(8,128)(2,1)} %param.3) | copy-start | bytes 4915204
  50.0 0.8 copy-start.1
Sparse Core Ops, SparseCore 0:
  50.1 82.9 reduce-scatter.3
